TPU v7x, 512 devices: a whole 4x8x8 slice. The times are simulated.
512 devices in a mesh: section: 8 (over z), expert: 16 (over y, core), dp: 4 (over x).
Axes of the slice: x: 4, y: 8, z: 8, core: 2. Of those that a mesh axis runs over, the one named last changes fastest.
Arguments:
- arrivals: bfloat16 [8, 4096, 2048], P('section', ('expert', 'dp')), may hold values from -6 to 6
- fresh: bfloat16 [1, 4096, 2048], P(None, ('expert', 'dp')), may hold values from -6 to 6
- routes: int32 [8, 2, 4096, 6], P('section', None, ('expert', 'dp')), may hold values from 0 to 63, as said below
- gates: bfloat16 [8, 2, 4096, 6], P('section', None, ('expert', 'dp')), may hold values from 0.099609375 to 1
- cotangent: bfloat16 [8, 2, 4096, 2048], P('section', None, ('expert', 'dp')), may hold values from -0.3125 to 0.3125
- norm_gain: float32 [8, 2048], P('section'), may hold values from 0.5 to 1.5
- w_gate: bfloat16 [8, 5632, 2048], P('section', 'expert', 'dp'), may hold values from -0.125 to 0.125
- w_up: bfloat16 [8, 5632, 2048], P('section', 'expert', 'dp'), may hold values from -0.125 to 0.125
- w_down: bfloat16 [8, 5632, 2048], P('section', 'expert', 'dp'), may hold values from -0.15625 to 0.15625
Outputs:
- layer_out: bfloat16 [8, 2, 4096, 2048], P('section', None, ('expert', 'dp'))
- grad_down: float32 [8, 5632, 2048], P('section', 'expert', 'dp')
Inputs may be any that keep to these rules, and one draw needn't show every extreme that they name: `routes`: each token's 6 entries are different expert numbers.
All inputs are finite; a program needn't handle non-finite values.
Results may differ from a plain program's by a relative error of at most 0.0085.
Values may be sent and summed in bfloat16 or wider, within the bound.
A program may use at most 64 MiB of HBM per device.

v0:
```python
import functools

import jax
import jax.numpy as jnp
from jax import lax
from jax.experimental import pallas as pl
from jax.experimental.pallas import tpu as pltpu
from jax.sharding import PartitionSpec as P

SPLIT = 4
CAP = 12
SLOTS = 16
CORES = 2
PAIRS = SPLIT // CORES
MESH = pl.DeviceIdType.MESH
BF = jnp.bfloat16
F32 = jnp.float32

TOK, COT, CROSS, SWAP, HID, RET, PICK, BASE, BACK, SEMS = 0, 8, 10, 12, 14, 16, 27, 28, 29, 30
NEAR, NEXT, RING, WRAP, CROSSED, TWIN, READY = 0, 4, 5, 6, 7, 8, 9


def mm(a, b, ca=1, cb=0):
    return lax.dot_general(a, b, (((ca,), (cb,)), ((), ())), preferred_element_type=F32)


def kernel(
    n_s, n_e, n_d, steps,
    arr_h, fresh_h, routes_h, gates_h, cot_h, gain_h, wg_h, wu_h, wd_h,
    out, grad,
    wg, wu, wd, routes, gates, gain, cot, fresh, inc, base,
    toks, tokr, cots, cotr, cotx, xg, acc, hid_s, hidr, hp, rets, retr,
    pick_s, pick_r, back,
    load_sems, w_send, w_recv, d_send, d_recv, send_sems, recv_sems, ready,
):
    sec = lax.axis_index("section")
    exp = lax.axis_index("expert")
    dp = lax.axis_index("dp")
    n_y = n_e // CORES
    flight = n_e // SPLIT
    n_c, rows, cols = inc.shape[1:]
    half = cols // 2
    units = wd.shape[3]
    part_units = units // 2
    width = cols * n_c
    used = flight * SLOTS
    n_low = 8 * n_y
    core = lax.rem(exp, CORES)
    y = exp // CORES
    sibling = (sec, exp + 1 - 2 * core, dp)
    nxt = lax.rem(sec + 1, n_s)
    prv = lax.rem(sec + n_s - 1, n_s)
    right = lax.rem(dp + 1, n_d)
    left = lax.rem(dp + n_d - 1, n_d)
    opp = lax.rem(dp + 2, n_d)
    to_right = (sec, exp, right)
    to_left = (sec, exp, left)
    to_next = (nxt, exp, dp)
    to_prev = (prv, exp, dp)
    offs = sorted(range(1, n_y), key=lambda o: -min(o, n_y - o))
    last = steps - 1

    def row(o):
        return lax.rem(y + o, n_y)

    above = (sec, row(1) * CORES + core, dp)
    below = (sec, row(n_y - 1) * CORES + core, dp)
    first_sec = sec == 0
    last_sec = sec == n_s - 1

    barrier = pltpu.get_barrier_semaphore()

    def signal(target):
        pl.semaphore_signal(barrier, inc=1, device_id=target, device_id_type=MESH)

    for target in (to_right, to_left, sibling, above, below):
        signal(target)

    @pl.when(jnp.logical_not(last_sec))
    def _():
        signal(to_next)

    @pl.when(first_sec)
    def _():
        signal(to_prev)

    greeted = 5 + jnp.minimum(sec, 1) + sec // (n_s - 1)

    def tell(i, *targets):
        for target in targets:
            pl.semaphore_signal(ready.at[i], inc=1, device_id=target, device_id_type=MESH)

    def told(i, n):
        pl.semaphore_wait(ready.at[i], n)

    def ring(i):
        told(NEAR + i, 2)
        if i < 3:
            tell(NEAR + i + 1, above, below)

    loads = []

    def load(src, dst):
        copy = pltpu.make_async_copy(src, dst, load_sems.at[len(loads)])
        copy.start()
        loads.append(copy)
        return copy

    def piece(c):
        return pl.ds(c * cols, cols)

    subs = range(n_c)
    load_w = [load(wg_h.at[0], wg.at[core, dp]), load(wu_h.at[0], wu.at[core, dp])]
    load_r = [load(routes_h, routes), load(gates_h, gates)]
    load_a = [load(arr_h.at[0, :, piece(c)], inc.at[0, c]) for c in subs]
    load_d = [load(wd_h.at[0, :, piece(q)], wd.at[core, dp, q]) for q in range(2)]
    load_c = load(cot_h, cot)
    load_g = [load(gain_h.at[:, piece(c)], gain.at[c]) for c in subs]
    load_f = [load(fresh_h.at[0, :, piece(c)], fresh.at[c]) for c in subs]

    def remote(src, dst, sem, target):
        return pltpu.make_async_remote_copy(
            src_ref=src, dst_ref=dst, send_sem=send_sems.at[sem], recv_sem=recv_sems.at[sem],
            device_id=target, device_id_type=MESH,
        )

    def got(ref, sem):
        remote(ref, ref, sem, sibling).wait_recv()

    def sent(ref, sem):
        remote(ref, ref, sem, sibling).wait_send()

    mats = (wg, wu)

    def w_copy(ref, m, i, target):
        return pltpu.make_async_remote_copy(
            src_ref=ref, dst_ref=ref, send_sem=w_send.at[m, i], recv_sem=w_recv.at[m, i],
            device_id=target, device_id_type=MESH,
        )

    def w_own(m):
        load_w[m].wait()
        mine = mats[m].at[core, dp]
        w_copy(mine, m, 0, to_right).start()
        w_copy(mine, m, 1, to_left).start()
        w_copy(mine, m, 4, sibling).start()

    def w_pass(m):
        w = mats[m]
        w_copy(w.at[core, left], m, 0, sibling).wait_recv()
        w_copy(w.at[core, left, pl.ds(0, part_units)], m, 2, to_right).start()
        w_copy(w.at[core, left], m, 5, sibling).start()
        w_copy(w.at[core, right], m, 1, sibling).wait_recv()
        w_copy(w.at[core, right, pl.ds(part_units, part_units)], m, 3, to_left).start()
        w_copy(w.at[core, right], m, 6, sibling).start()

    def w_last(m):
        for h in range(2):
            ref = mats[m].at[core, opp, pl.ds(h * part_units, part_units)]
            w_copy(ref, m, 2 + h, sibling).wait_recv()
            w_copy(ref, m, 7 + h, sibling).start()

    def w_twin(m, i):
        if i < 3:
            w_copy(mats[m].at[1 - core, (dp, left, right)[i]], m, 4 + i, sibling).wait_recv()
        else:
            for h in range(2):
                ref = mats[m].at[1 - core, opp, pl.ds(h * part_units, part_units)]
                w_copy(ref, m, 7 + h, sibling).wait_recv()

    def d_copy(ref, i, target):
        return pltpu.make_async_remote_copy(
            src_ref=ref, dst_ref=ref, send_sem=d_send.at[i], recv_sem=d_recv.at[i],
            device_id=target, device_id_type=MESH,
        )

    def d_own():
        for q in range(2):
            load_d[q].wait()
            d_copy(wd.at[core, dp, q], q, to_right).start()
            d_copy(wd.at[core, dp, q], 2 + q, to_left).start()
        d_copy(wd.at[core, dp], 8, sibling).start()

    def d_pass(q):
        d_copy(wd.at[core, left, q], q, sibling).wait_recv()
        d_copy(wd.at[core, left, q, pl.ds(0, part_units)], 4 + q, to_right).start()
        d_copy(wd.at[core, left, q], 10 + q, sibling).start()
        d_copy(wd.at[core, right, q], 2 + q, sibling).wait_recv()
        d_copy(wd.at[core, right, q, pl.ds(part_units, part_units)], 6 + q, to_left).start()
        d_copy(wd.at[core, right, q], 12 + q, sibling).start()

    def d_last(q):
        for h in range(2):
            ref = wd.at[core, opp, q, pl.ds(h * part_units, part_units)]
            d_copy(ref, 4 + 2 * h + q, sibling).wait_recv()
            d_copy(ref, 14 + 2 * q + h, sibling).start()

    def d_twin(name, q):
        if name == "own":
            d_copy(wd.at[1 - core, dp], 8, sibling).wait_recv()
        elif name == "left":
            d_copy(wd.at[1 - core, left, q], 10 + q, sibling).wait_recv()
        elif name == "right":
            d_copy(wd.at[1 - core, right, q], 12 + q, sibling).wait_recv()
        else:
            for h in range(2):
                ref = wd.at[1 - core, opp, q, pl.ds(h * part_units, part_units)]
                d_copy(ref, 14 + 2 * q + h, sibling).wait_recv()

    lane = lax.broadcasted_iota(jnp.int32, (used, rows), 0)
    lane_expert = lane >> 4
    lane_slot = lane & (SLOTS - 1)
    t_row = lax.broadcasted_iota(jnp.int32, (rows, rows), 0)
    t_col = lax.broadcasted_iota(jnp.int32, (rows, rows), 1)
    earlier_tok = jnp.where(t_row < t_col, 1.0, 0.0).astype(BF)

    def selection(k):
        naming = jnp.zeros((used, rows), F32)
        shares = jnp.zeros((used, rows), F32)
        for j in range(routes.shape[1]):
            hit = routes[0, j, k:k + 1, :] == lane_expert
            naming = jnp.where(hit, 1.0, naming)
            shares = shares + jnp.where(hit, gates[0, j].astype(F32)[k:k + 1, :], 0.0)
        places = mm(naming.astype(BF), earlier_tok)
        chosen = jnp.where(places == lane_slot.astype(F32), naming, 0.0)
        chosen = jnp.where(lane_slot < CAP, chosen, 0.0)
        return chosen.astype(BF), (chosen * shares).astype(BF)

    r_i = lax.broadcasted_iota(jnp.int32, (CAP * n_y, n_low), 0)
    c_i = lax.broadcasted_iota(jnp.int32, (CAP * n_y, n_low), 1)
    c_slot = c_i & 7
    shift = r_i - (c_i >> 3) * CAP - c_slot
    low_rows = jnp.where(shift == 0, 1.0, 0.0)
    tail_a = jnp.where((shift == 8) & (c_slot < 4), 1.0, 0.0)
    tail_b = jnp.where((shift == 4) & (c_slot >= 4), 1.0, 0.0)
    layout = jnp.concatenate([low_rows, tail_a, tail_b], axis=1).astype(BF)
    blank = jnp.zeros((n_low, half), BF)

    def swap(block):
        return jnp.concatenate([block[4:], block[:4]], axis=0)

    def fill(store, k, c, block):
        for f in range(flight):
            top = block[f * SLOTS:f * SLOTS + 8]
            bottom = block[f * SLOTS + 8:(f + 1) * SLOTS]
            store[k, c, f, :, :cols] = top.astype(BF)
            store[k, c, f, :, cols:] = (bottom[:, :half] + swap(bottom[:, half:])).astype(BF)

    def unpack(landing, *at):
        flat = landing[at].reshape(n_low, cols + half)
        tail = flat[:, cols:]
        stacked = jnp.concatenate(
            [
                flat[:, :cols],
                jnp.concatenate([tail, blank], axis=1),
                jnp.concatenate([blank, tail], axis=1),
            ],
            axis=0,
        )
        return mm(layout, stacked)

    def spread_all(store, landing, k, sem):
        for o in offs:
            remote(
                store.at[k, pl.ds(0, n_c), row(o) // PAIRS],
                landing.at[k, pl.ds(0, n_c), y], sem, (sec, row(o) * CORES + core, dp),
            ).start()
        for c in subs:
            landing[k, c, y] = store[k, c, y // PAIRS]

    def spread_some(store, landing, k, sub, n, sem):
        for o in offs:
            remote(
                store.at[k, pl.ds(sub, n), row(o) // PAIRS], landing.at[k, pl.ds(sub, n), y],
                sem, (sec, row(o) * CORES + core, dp),
            ).start()
        for q in range(n):
            landing[k, sub + q, y] = store[k, sub + q, y // PAIRS]

    def prepare(k, c):
        block = unpack(tokr, k, c)
        xg[c] = (block * gain[c]).astype(BF)
        return jnp.sum(block * block, axis=1, keepdims=True)

    def contract(parts, first, cores):
        for c in cores:
            for i, w in enumerate(mats):
                total = sum(
                    mm(xg[2 * ch + q], w[c, ch, :, q * cols:(q + 1) * cols], 1, 1)
                    for ch, q in parts
                )
                acc[i, c] = total if first else acc[i, c] + total

    def send_hidden(k):
        slot = hidr.at[k, core * n_d + dp]
        for x in (opp, right, left):
            for c in range(CORES):
                there = y * CORES + c
                remote(hid_s.at[k, c], slot, HID + k, (sec, there, x)).start()
        remote(hid_s.at[k, 1 - core], slot, HID + k, sibling).start()
        hidr[k, core * n_d + dp] = hid_s[k, core]

    def activate(k, squares, early):
        scale = lax.rsqrt(squares * (1.0 / width) + 0.5)
        for c in range(CORES):
            act_g = acc[0, c] * scale
            hid_s[k, c] = (act_g / (1.0 + jnp.exp(-act_g)) * (acc[1, c] * scale)).astype(BF)
        if early:
            send_hidden(k)
        for c in range(CORES):
            hp[c] = mm(layout, hid_s[k, c], 0, 0).astype(BF)

    def down(k, ch, qs, i, late=None):
        sub = 2 * ch + qs[0]
        for q in qs:
            rows_out = mm(hp[core], wd[core, ch, q])
            if late is not None and q == qs[0]:
                d_twin(late, q)
            rows_out = rows_out + mm(hp[1 - core], wd[1 - core, ch, q])
            tail = rows_out[n_low:2 * n_low, :half] + rows_out[2 * n_low:, half:]
            rets[k, 2 * ch + q, :, :, :cols] = rows_out[:n_low].astype(BF).reshape(n_y, 8, cols)
            rets[k, 2 * ch + q, :, :, cols:] = tail.astype(BF).reshape(n_y, 8, half)
        there = sec if k == last else nxt
        span = pl.ds(sub, len(qs))
        for o in offs + ([] if k == last else [0]):
            remote(
                rets.at[k, span, row(o)], retr.at[k, span, y], RET + 7 * k + i,
                (there, row(o) * CORES + core, dp),
            ).start()
        if k == last:
            for q in qs:
                retr[k, 2 * ch + q, y] = rets[k, 2 * ch + q, y]

    row_8 = lax.broadcasted_iota(jnp.int32, (8, half), 0)

    def landed(k, ch, qs, i):
        n = n_y - 1 if k == last else n_y
        got(retr.at[k, pl.ds(2 * ch + qs[0], len(qs)), pl.ds(0, n)], RET + 7 * k + i)

    def combine(k, c, weights, inputs):
        tops = []
        for f in range(flight):
            total = sum(retr[k, c, f * PAIRS + p].astype(F32) for p in range(PAIRS))
            tail = total[:, cols:]
            tops.append(total[:, :cols])
            tops.append(jnp.concatenate(
                [jnp.where(row_8 < 4, tail, 0.0), jnp.where(row_8 < 4, swap(tail), 0.0)], axis=1
            ))
        mixed = jnp.concatenate(tops, axis=0)
        high = mixed.astype(BF)
        low = (mixed - high.astype(F32)).astype(BF)
        mixture = mm(weights, high, 0, 0) + mm(weights, low, 0, 0)
        return (inputs.astype(F32) + mixture).astype(BF)

    def at_cols(c):
        return pl.ds(pl.multiple_of(c * cols, cols), cols)

    pl.semaphore_wait(barrier, greeted)
    w_own(0)
    w_own(1)
    tell(NEAR, above, below)
    tell(CROSSED, to_right, to_left)

    @pl.when(jnp.logical_not(first_sec))
    def _():
        tell(NEXT, to_prev)

    @pl.when(last_sec)
    def _():
        tell(WRAP, to_next)

    for copy in load_r:
        copy.wait()
    picks = [selection(0)]
    pick_s[...] = picks[0][1]
    for copy in load_a:
        copy.wait()
    ring(0)
    told(CROSSED, 2)
    tell(TWIN, sibling)
    for c in subs:
        fill(toks, 0, c, mm(picks[0][0], inc[0, c]))
    ring(1)
    picks.append(selection(1))
    load_c.wait()
    for c in subs:
        fill(cots, 0, c, mm(picks[0][1], cot[0, 0, :, c * cols:(c + 1) * cols]))
    ring(2)

    @pl.when(jnp.logical_not(first_sec))
    def _():
        tell(RING, to_prev)

    spread_all(toks, tokr, 0, TOK)
    spread_all(cots, cotr, 0, COT)
    for c in subs:
        fill(cots, 1, c, mm(picks[1][1], cot[0, 1, :, c * cols:(c + 1) * cols]))
    spread_all(cots, cotr, 1, COT + 1)

    @pl.when(jnp.logical_not(last_sec))
    def _():
        told(NEXT, 1)

    remote(inc.at[0], base, BASE, to_next).start()
    remote(pick_s, pick_r, PICK, to_next).start()
    for copy in load_g + load_f:
        copy.wait()
    told(TWIN, 1)

    items = (
        (dp, (0, 1)), (right, (0,)), (left, (0,)), (right, (1,)), (left, (1,)),
        (opp, (0,)), (opp, (1,)),
    )

    def enter(i, blocks):
        ch, qs = items[i]
        for q, block in zip(qs, blocks):
            inc[1, 2 * ch + q] = block
            fill(toks, 1, 2 * ch + q, mm(picks[1][0], block))
        spread_some(toks, tokr, 1, 2 * ch + qs[0], len(qs), TOK + 1 + i)

    def settle(i):
        ch, qs = items[i]
        landed(0, ch, qs, i)
        results = []
        for q in qs:
            c = 2 * ch + q
            results.append(combine(0, c, pick_r[...], base[c]))
            back[c] = results[-1]
            remote(back.at[c], out.at[0, 0, :, at_cols(c)], BACK, to_prev).start()
        return results

    def relay(i):
        ch, qs = items[i]

        @pl.when(first_sec)
        def _():
            enter(i, [fresh[2 * ch + q] for q in qs])

        @pl.when(jnp.logical_not(first_sec))
        def _():
            enter(i, settle(i))

    def tok_in(i):
        ch, qs = items[i]
        got(tokr.at[1, pl.ds(2 * ch + qs[0], len(qs)), pl.ds(0, n_y - 1)], TOK + 1 + i)
        return sum(prepare(1, 2 * ch + q) for q in qs)

    def parts_of(*which):
        return [(items[i][0], q) for i in which for q in items[i][1]]

    near = parts_of(0, 1, 2, 3, 4)
    far = parts_of(5, 6)
    w_pass(0)
    got(tokr.at[0, pl.ds(0, n_c), pl.ds(0, n_y - 1)], TOK)
    squares = sum(prepare(0, c) for c in subs)
    w_pass(1)
    d_own()
    contract(near, True, (core,))
    for m in range(2):
        for i in range(3):
            w_twin(m, i)
    contract(near, True, (1 - core,))
    w_last(0)
    w_last(1)
    contract(far, False, (core,))
    w_twin(0, 3)
    w_twin(1, 3)
    contract(far, False, (1 - core,))
    activate(0, squares, False)
    ring(3)

    @pl.when(jnp.logical_not(last_sec))
    def _():
        told(RING, 1)

    down(0, dp, (0, 1), 0, "own")
    d_pass(0)
    d_twin("right", 0)
    down(0, right, (0,), 1)
    d_twin("left", 0)
    down(0, left, (0,), 2)
    got(base, BASE)
    got(pick_r, PICK)
    d_pass(1)
    relay(0)
    d_twin("right", 1)
    down(0, right, (1,), 3)
    d_twin("left", 1)
    down(0, left, (1,), 4)
    d_last(0)
    send_hidden(0)
    for k in range(steps):
        got(cotr.at[k, pl.ds(0, n_c), pl.ds(0, n_y - 1)], COT + k)
        for x in (opp, right, left):
            remote(
                cotr.at[k, pl.ds(2 * x, 2)], cotx.at[k, core, dp], CROSS + k, (sec, exp, x)
            ).start()
        for q in range(2):
            cotx[k, core, dp, q] = cotr[k, 2 * dp + q]
    down(0, opp, (0,), 5, "opp")
    d_last(1)
    relay(1)
    down(0, opp, (1,), 6, "opp")
    relay(2)
    relay(3)
    relay(4)
    squares = tok_in(0)
    relay(5)
    relay(6)
    squares = squares + tok_in(1) + tok_in(2)
    contract(parts_of(0, 1, 2), True, (0, 1))
    squares = squares + tok_in(3) + tok_in(4)
    squares = squares + tok_in(5)
    contract(parts_of(3, 4, 5), False, (0, 1))
    squares = squares + tok_in(6)
    contract(parts_of(6), False, (0, 1))
    activate(1, squares, True)
    order = (dp, right, left, opp)
    for i, ch in enumerate(order):
        down(1, ch, (0, 1), i)

    @pl.when(first_sec)
    def _():
        told(WRAP, 1)
        for i in range(len(items)):
            settle(i)

    for k in range(steps):
        got(cotx.at[k, core, pl.ds(0, n_d - 1)], CROSS + k)
        remote(cotx.at[k, core], cotx.at[k, core], SWAP + k, sibling).start()
    for k in range(steps):
        got(cotx.at[k, 0], SWAP + k)
        got(hidr.at[k, pl.ds(0, CORES * n_d - 1)], HID + k)
        total = 0.0
        for c in range(CORES):
            rows_cot = jnp.concatenate(
                [
                    jnp.concatenate(
                        [unpack(cotx, k, c, x, q).astype(BF) for q in range(2)], axis=1
                    )
                    for x in range(n_d)
                ],
                axis=0,
            )
            rows_hid = hidr[k, pl.ds(c * n_d, n_d)].reshape(n_d * CAP * n_y, units)
            total = total + mm(rows_hid, rows_cot, 0, 0)
        grad[0] = total if k == 0 else grad[0] + total
    for i, ch in enumerate(order):
        landed(1, ch, (0, 1), i)
        for q in range(2):
            c = 2 * ch + q
            out[0, 1, :, at_cols(c)] = combine(1, c, picks[1][1], inc[1, c])

    got(back, BACK)
    for m in range(2):
        w = mats[m]
        for i in (0, 1, 4, 5, 6):
            w_copy(w.at[0, 0], m, i, sibling).wait_send()
        for i in (2, 3, 7, 8):
            w_copy(w.at[0, 0, pl.ds(0, part_units)], m, i, sibling).wait_send()
    for i in (0, 1, 2, 3, 10, 11, 12, 13):
        d_copy(wd.at[0, 0, 0], i, sibling).wait_send()
    for i in (4, 5, 6, 7, 14, 15, 16, 17):
        d_copy(wd.at[0, 0, 0, pl.ds(0, part_units)], i, sibling).wait_send()
    d_copy(wd.at[0, 0], 8, sibling).wait_send()
    sent(tokr.at[0, pl.ds(0, n_c), pl.ds(0, n_y - 1)], TOK)
    for i, (ch, qs) in enumerate(items):
        sent(tokr.at[1, pl.ds(0, len(qs)), pl.ds(0, n_y - 1)], TOK + 1 + i)
        sent(rets.at[0, pl.ds(0, len(qs))], RET + i)
    for i in range(n_d):
        sent(rets.at[1, pl.ds(0, 2), pl.ds(0, n_y - 1)], RET + 7 + i)
    for k in range(steps):
        sent(cotr.at[k, pl.ds(0, n_c), pl.ds(0, n_y - 1)], COT + k)
        sent(cotx.at[k, 0, pl.ds(0, n_d - 1)], CROSS + k)
        sent(cotx.at[k, 0], SWAP + k)
        sent(hidr.at[k, pl.ds(0, CORES * n_d - 1)], HID + k)
    sent(pick_s, PICK)
    sent(base, BASE)
    sent(back, BACK)


def finish(out_in, grad_in, out, grad, sems):
    pieces = ((out_in, out), (grad_in, grad))
    copies = [pltpu.make_async_copy(src, dst, sems.at[i]) for i, (src, dst) in enumerate(pieces)]
    for copy in copies:
        copy.start()
    for copy in copies:
        copy.wait()


def local(sizes, arrivals, fresh, routes, gates, cotangent, norm_gain, w_gate, w_up, w_down):
    n_s, n_e, n_d = sizes
    steps = routes.shape[1]
    tok_rows, width = arrivals.shape[1:]
    units, cols = w_gate.shape[1:]
    flight = n_e // SPLIT
    n_y = n_e // CORES
    n_c = 2 * n_d
    rows = CAP * n_y
    used = flight * SLOTS
    sub = cols // 2
    packed = sub + sub // 2
    hbm = pl.BlockSpec(memory_space=pltpu.HBM)
    held = pl.BlockSpec(memory_space=pltpu.VMEM)

    def vmem(*shape, kind=BF):
        return pltpu.VMEM(shape, kind)

    dma = pltpu.SemaphoreType.DMA
    made = pl.pallas_call(
        functools.partial(kernel, n_s, n_e, n_d, steps),
        out_shape=(
            pltpu.VMEM((1, steps, tok_rows, width), BF),
            pltpu.VMEM((1, units, cols), F32),
        ),
        in_specs=[hbm] * 9,
        out_specs=(held, held),
        scratch_shapes=[
            vmem(CORES, n_d, units, cols),
            vmem(CORES, n_d, units, cols),
            vmem(CORES, n_d, 2, units, sub),
            vmem(1, routes.shape[3], steps, tok_rows, kind=jnp.int32),
            vmem(1, routes.shape[3], steps, tok_rows),
            vmem(n_c, 1, sub, kind=F32),
            vmem(*cotangent.shape),
            vmem(n_c, tok_rows, sub),
            vmem(steps, n_c, tok_rows, sub),
            vmem(n_c, tok_rows, sub),
            vmem(steps, n_c, flight, 8, packed),
            vmem(steps, n_c, n_y, 8, packed),
            vmem(steps, n_c, flight, 8, packed),
            vmem(steps, n_c, n_y, 8, packed),
            vmem(steps, CORES, n_d, 2, n_y, 8, packed),
            vmem(n_c, rows, sub),
            vmem(2, CORES, rows, units, kind=F32),
            vmem(steps, CORES, rows, units),
            vmem(steps, CORES * n_d, rows, units),
            vmem(CORES, 24 * n_y, units),
            vmem(steps, n_c, n_y, 8, packed),
            vmem(steps, n_c, n_y, 8, packed),
            vmem(used, tok_rows),
            vmem(used, tok_rows),
            vmem(n_c, tok_rows, sub),
            dma((7 + 3 * n_c,)),
            dma((2, 9)),
            dma((2, 9)),
            dma((18,)),
            dma((18,)),
            dma((SEMS,)),
            dma((SEMS,)),
            pltpu.SemaphoreType.REGULAR((READY,)),
        ],
        compiler_params=pltpu.CompilerParams(
            collective_id=0, has_side_effects=True, vmem_limit_bytes=64240 * 1024
        ),
    )(
        arrivals, fresh, jnp.transpose(routes, (0, 3, 1, 2)),
        jnp.transpose(gates, (0, 3, 1, 2)), cotangent,
        norm_gain, w_gate, w_up, w_down,
    )
    return pl.pallas_call(
        finish,
        out_shape=tuple(jax.ShapeDtypeStruct(m.shape, m.dtype) for m in made),
        in_specs=[held] * 2,
        out_specs=(hbm, hbm),
        scratch_shapes=[pltpu.SemaphoreType.DMA((2,))],
        compiler_params=pltpu.CompilerParams(vmem_limit_bytes=4096 * 1024),
    )(*made)


def solution(mesh):
    placed = (
        P("section", ("expert", "dp"), None),
        P(None, ("expert", "dp"), None),
        P("section", None, ("expert", "dp"), None),
        P("section", None, ("expert", "dp"), None),
        P("section", None, ("expert", "dp"), None),
        P("section", None),
        P("section", "expert", "dp"),
        P("section", "expert", "dp"),
        P("section", "expert", "dp"),
    )
    sizes = (mesh.shape["section"], mesh.shape["expert"], mesh.shape["dp"])
    return jax.shard_map(
        functools.partial(local, sizes),
        mesh=mesh,
        in_specs=placed,
        out_specs=(P("section", None, ("expert", "dp"), None), P("section", "expert", "dp")),
        check_vma=False,
    )
```

profile of v0, /device:TPU:1, one launch (start us, length us, event | category | flops | bytes accessed | tf_op | source)
XLA Modules:
  0.0 72.5 jit_solution(11357605549363016952)
XLA Ops:
  0.6 70.8 %shard_map.104 = (bf16[1,2,64,2048]{3,2,1,0:T(8,128)(2,1)S(1)}, f32[1,352,512]{2,1,0:T(8,128)S(1)}) custom-call(bf16[1,64,2048]{2,1,0:T(8,128)(2,1)} %arr_h.1, bf16[1,64,2048]{2,1,0:T(8,128)(2,1)} %fresh_h.1, s32[1,6,2,64]{3,2,1,0:T(2,128)} %bitcast.2, bf16[1,6,2,64]{3,2,1,0:T(2,128)(2,1)} %bitcast.3, bf16[1,2,64,2048]{3,2,1,0:T(8,128)(2,1)} %cot_h.1, ...), custom_call_target="tpu_custom_call" | custom-call | tf_op jit(solution)/shard_map/pallas_call | solution.py:611
  71.5 1.1 %shard_map.105 = (bf16[1,2,64,2048]{3,2,1,0:T(8,128)(2,1)}, f32[1,352,512]{2,1,0:T(8,128)}) custom-call(bf16[1,2,64,2048]{3,2,1,0:T(8,128)(2,1)S(1)} %get-tuple-element.4.out_in, f32[1,352,512]{2,1,0:T(8,128)S(1)} %get-tuple-element.5.grad_in), custom_call_target="tpu_custom_call" | custom-call | tf_op jit(solution)/shard_map/pallas_call | solution.py:662
where the time goes:
time: 72.6 us; the launch traced here: 72.5 us
  Pallas kernels  71.9 us (99%)
    pallas_call x1, Pallas kernels, local(): pl.pallas_call(functools.partial(kernel, n_s, n_e, n_d, steps), out_shape...  70.8 us

commit v1 on v0

--- a/solution.py
+++ b/solution.py
@@ -16,7 +16,8 @@
 BF = jnp.bfloat16
 F32 = jnp.float32
 
-TOK, COT, CROSS, SWAP, HID, RET, PICK, BASE, BACK, SEMS = 0, 8, 10, 12, 14, 16, 27, 28, 29, 30
+TOK, COT, CROSS, SWAP, HID, RET, PICK, BASE, BACK, PART, OVER, SEMS = 0, 8, 10, 12, 14, 16, 27, 28, 29, 30, 34, 35
+SENDS = 10
 NEAR, NEXT, RING, WRAP, CROSSED, TWIN, READY = 0, 4, 5, 6, 7, 8, 9
 
 
@@ -31,16 +32,16 @@
     wg, wu, wd, routes, gates, gain, cot, fresh, inc, base,
     toks, tokr, cots, cotr, cotx, xg, acc, hid_s, hidr, hp, rets, retr,
     pick_s, pick_r, back,
-    load_sems, w_send, w_recv, d_send, d_recv, send_sems, recv_sems, ready,
+    load_sems, w_send, w_recv, d_recv, send_sems, recv_sems, ready,
 ):
     sec = lax.axis_index("section")
     exp = lax.axis_index("expert")
     dp = lax.axis_index("dp")
     n_y = n_e // CORES
     flight = n_e // SPLIT
-    n_c, rows, cols = inc.shape[1:]
+    n_c, rows, cols = back.shape
     half = cols // 2
-    units = wd.shape[3]
+    units = wd.shape[2]
     part_units = units // 2
     width = cols * n_c
     used = flight * SLOTS
@@ -106,106 +107,113 @@
         loads.append(copy)
         return copy
 
+    def at_cols(c):
+        return pl.ds(pl.multiple_of(c * cols, cols), cols)
+
     def piece(c):
         return pl.ds(c * cols, cols)
 
     subs = range(n_c)
-    load_w = [load(wg_h.at[0], wg.at[core, dp]), load(wu_h.at[0], wu.at[core, dp])]
+    mine = core * n_d + dp
+    theirs = (1 - core) * n_d
+
+    def own(x):
+        return core * n_d + x
+
+    load_w = [load(wg_h.at[0], wg.at[mine]), load(wu_h.at[0], wu.at[mine])]
     load_r = [load(routes_h, routes), load(gates_h, gates)]
-    load_a = [load(arr_h.at[0, :, piece(c)], inc.at[0, c]) for c in subs]
-    load_d = [load(wd_h.at[0, :, piece(q)], wd.at[core, dp, q]) for q in range(2)]
+    load_a = load(arr_h.at[0], inc.at[0])
+    load_d = [load(wd_h.at[0, :, piece(q)], wd.at[mine, q]) for q in range(2)]
     load_c = load(cot_h, cot)
-    load_g = [load(gain_h.at[:, piece(c)], gain.at[c]) for c in subs]
-    load_f = [load(fresh_h.at[0, :, piece(c)], fresh.at[c]) for c in subs]
+    load_g = load(gain_h, gain)
+    load_f = load(fresh_h.at[0], fresh)
+
+    def send_of(sem):
+        firsts = (TOK, COT, CROSS, SWAP, HID, RET, RET + 7, PICK, BASE, BACK)
+        if sem >= PART:
+            return firsts.index(COT if sem < OVER else HID)
+        return max(i for i, first in enumerate(firsts) if sem >= first)
 
     def remote(src, dst, sem, target):
         return pltpu.make_async_remote_copy(
-            src_ref=src, dst_ref=dst, send_sem=send_sems.at[sem], recv_sem=recv_sems.at[sem],
+            src_ref=src, dst_ref=dst, send_sem=send_sems.at[send_of(sem)],
+            recv_sem=recv_sems.at[sem], device_id=target, device_id_type=MESH,
+        )
+
+    def got(ref, sem):
+        remote(ref, ref, sem, sibling).wait_recv()
+
+    def sent(ref, sem):
+        remote(ref, ref, sem, sibling).wait_send()
+
+    mats = (wg, wu)
+
+    def w_copy(ref, m, i, target):
+        return pltpu.make_async_remote_copy(
+            src_ref=ref, dst_ref=ref, send_sem=w_send.at[m], recv_sem=w_recv.at[m, i],
             device_id=target, device_id_type=MESH,
         )
 
-    def got(ref, sem):
-        remote(ref, ref, sem, sibling).wait_recv()
-
-    def sent(ref, sem):
-        remote(ref, ref, sem, sibling).wait_send()
-
-    mats = (wg, wu)
-
-    def w_copy(ref, m, i, target):
-        return pltpu.make_async_remote_copy(
-            src_ref=ref, dst_ref=ref, send_sem=w_send.at[m, i], recv_sem=w_recv.at[m, i],
-            device_id=target, device_id_type=MESH,
-        )
-
     def w_own(m):
         load_w[m].wait()
-        mine = mats[m].at[core, dp]
-        w_copy(mine, m, 0, to_right).start()
-        w_copy(mine, m, 1, to_left).start()
-        w_copy(mine, m, 4, sibling).start()
+        ref = mats[m].at[mine]
+        w_copy(ref, m, 0, to_right).start()
+        w_copy(ref, m, 1, to_left).start()
+        w_copy(ref, m, 3, sibling).start()
 
     def w_pass(m):
         w = mats[m]
-        w_copy(w.at[core, left], m, 0, sibling).wait_recv()
-        w_copy(w.at[core, left, pl.ds(0, part_units)], m, 2, to_right).start()
-        w_copy(w.at[core, left], m, 5, sibling).start()
-        w_copy(w.at[core, right], m, 1, sibling).wait_recv()
-        w_copy(w.at[core, right, pl.ds(part_units, part_units)], m, 3, to_left).start()
-        w_copy(w.at[core, right], m, 6, sibling).start()
+        w_copy(w.at[own(left)], m, 0, sibling).wait_recv()
+        w_copy(w.at[own(left), pl.ds(0, part_units)], m, 2, to_right).start()
+        w_copy(w.at[own(left)], m, 3, sibling).start()
+        w_copy(w.at[own(right)], m, 1, sibling).wait_recv()
+        w_copy(w.at[own(right), pl.ds(part_units, part_units)], m, 2, to_left).start()
+        w_copy(w.at[own(right)], m, 3, sibling).start()
 
     def w_last(m):
-        for h in range(2):
-            ref = mats[m].at[core, opp, pl.ds(h * part_units, part_units)]
-            w_copy(ref, m, 2 + h, sibling).wait_recv()
-            w_copy(ref, m, 7 + h, sibling).start()
-
-    def w_twin(m, i):
-        if i < 3:
-            w_copy(mats[m].at[1 - core, (dp, left, right)[i]], m, 4 + i, sibling).wait_recv()
+        ref = mats[m].at[own(opp)]
+        w_copy(ref, m, 2, sibling).wait_recv()
+        w_copy(ref, m, 4, sibling).start()
+
+    def w_twin(m, far_one):
+        if far_one:
+            w_copy(mats[m].at[theirs + opp], m, 4, sibling).wait_recv()
         else:
-            for h in range(2):
-                ref = mats[m].at[1 - core, opp, pl.ds(h * part_units, part_units)]
-                w_copy(ref, m, 7 + h, sibling).wait_recv()
+            w_copy(mats[m].at[pl.ds(theirs, 3)], m, 3, sibling).wait_recv()
 
     def d_copy(ref, i, target):
         return pltpu.make_async_remote_copy(
-            src_ref=ref, dst_ref=ref, send_sem=d_send.at[i], recv_sem=d_recv.at[i],
+            src_ref=ref, dst_ref=ref, send_sem=w_send.at[2], recv_sem=d_recv.at[i],
             device_id=target, device_id_type=MESH,
         )
 
     def d_own():
         for q in range(2):
             load_d[q].wait()
-            d_copy(wd.at[core, dp, q], q, to_right).start()
-            d_copy(wd.at[core, dp, q], 2 + q, to_left).start()
-        d_copy(wd.at[core, dp], 8, sibling).start()
+            d_copy(wd.at[mine, q], q, to_right).start()
+            d_copy(wd.at[mine, q], 2 + q, to_left).start()
+        d_copy(wd.at[mine], 6, sibling).start()
 
     def d_pass(q):
-        d_copy(wd.at[core, left, q], q, sibling).wait_recv()
-        d_copy(wd.at[core, left, q, pl.ds(0, part_units)], 4 + q, to_right).start()
-        d_copy(wd.at[core, left, q], 10 + q, sibling).start()
-        d_copy(wd.at[core, right, q], 2 + q, sibling).wait_recv()
-        d_copy(wd.at[core, right, q, pl.ds(part_units, part_units)], 6 + q, to_left).start()
-        d_copy(wd.at[core, right, q], 12 + q, sibling).start()
+        d_copy(wd.at[own(left), q], q, sibling).wait_recv()
+        d_copy(wd.at[own(left), q, pl.ds(0, part_units)], 4 + q, to_right).start()
+        d_copy(wd.at[own(left), q], 7 + q, sibling).start()
+        d_copy(wd.at[own(right), q], 2 + q, sibling).wait_recv()
+        d_copy(wd.at[own(right), q, pl.ds(part_units, part_units)], 4 + q, to_left).start()
+        d_copy(wd.at[own(right), q], 7 + q, sibling).start()
 
     def d_last(q):
-        for h in range(2):
-            ref = wd.at[core, opp, q, pl.ds(h * part_units, part_units)]
-            d_copy(ref, 4 + 2 * h + q, sibling).wait_recv()
-            d_copy(ref, 14 + 2 * q + h, sibling).start()
+        ref = wd.at[own(opp), q]
+        d_copy(ref, 4 + q, sibling).wait_recv()
+        d_copy(ref, 9 + q, sibling).start()
 
     def d_twin(name, q):
         if name == "own":
-            d_copy(wd.at[1 - core, dp], 8, sibling).wait_recv()
-        elif name == "left":
-            d_copy(wd.at[1 - core, left, q], 10 + q, sibling).wait_recv()
-        elif name == "right":
-            d_copy(wd.at[1 - core, right, q], 12 + q, sibling).wait_recv()
+            d_copy(wd.at[theirs + dp], 6, sibling).wait_recv()
+        elif name == "near":
+            d_copy(wd.at[theirs + dp], 7 + q, sibling).wait_recv()
         else:
-            for h in range(2):
-                ref = wd.at[1 - core, opp, q, pl.ds(h * part_units, part_units)]
-                d_copy(ref, 14 + 2 * q + h, sibling).wait_recv()
+            d_copy(wd.at[theirs + opp, q], 9 + q, sibling).wait_recv()
 
     lane = lax.broadcasted_iota(jnp.int32, (used, rows), 0)
     lane_expert = lane >> 4
@@ -259,46 +267,51 @@
         )
         return mm(layout, stacked)
 
-    def spread_all(store, landing, k, sem):
-        for o in offs:
-            remote(
-                store.at[k, pl.ds(0, n_c), row(o) // PAIRS],
-                landing.at[k, pl.ds(0, n_c), y], sem, (sec, row(o) * CORES + core, dp),
-            ).start()
-        for c in subs:
-            landing[k, c, y] = store[k, c, y // PAIRS]
-
-    def spread_some(store, landing, k, sub, n, sem):
-        for o in offs:
+    def spread(store, landing, k, sem, targets, sub=0, n=None):
+        n = n_c if n is None else n
+        for o in targets:
             remote(
                 store.at[k, pl.ds(sub, n), row(o) // PAIRS], landing.at[k, pl.ds(sub, n), y],
                 sem, (sec, row(o) * CORES + core, dp),
             ).start()
+
+    def keep(store, landing, k, sub, n):
         for q in range(n):
             landing[k, sub + q, y] = store[k, sub + q, y // PAIRS]
 
     def prepare(k, c):
         block = unpack(tokr, k, c)
-        xg[c] = (block * gain[c]).astype(BF)
+        xg[c] = (block * gain[:, at_cols(c)]).astype(BF)
         return jnp.sum(block * block, axis=1, keepdims=True)
 
-    def contract(parts, first, cores):
+    def contract(parts, first, cores, which=(0, 1)):
         for c in cores:
-            for i, w in enumerate(mats):
+            for i in which:
+                w = mats[i]
                 total = sum(
-                    mm(xg[2 * ch + q], w[c, ch, :, q * cols:(q + 1) * cols], 1, 1)
+                    mm(xg[2 * ch + q], w[c * n_d + ch, :, q * cols:(q + 1) * cols], 1, 1)
                     for ch, q in parts
                 )
                 acc[i, c] = total if first else acc[i, c] + total
 
     def send_hidden(k):
-        slot = hidr.at[k, core * n_d + dp]
-        for x in (opp, right, left):
+        slot = hidr.at[k, mine]
+        for x in (opp, right, left)[0 if k == last else 1:]:
             for c in range(CORES):
                 there = y * CORES + c
                 remote(hid_s.at[k, c], slot, HID + k, (sec, there, x)).start()
-        remote(hid_s.at[k, 1 - core], slot, HID + k, sibling).start()
-        hidr[k, core * n_d + dp] = hid_s[k, core]
+        remote(hid_s.at[k, 1 - core], slot, HID + k if k == last else OVER, sibling).start()
+        hidr[k, mine] = hid_s[k, core]
+
+    half_rows = CAP * n_y // 2
+
+    def pass_hidden():
+        got(hidr.at[0, pl.ds(0, 2 * CORES)], HID)
+        for c in range(CORES):
+            upper = hidr.at[0, c * n_d + left, pl.ds(0, half_rows)]
+            lower = hidr.at[0, c * n_d + right, pl.ds(half_rows, half_rows)]
+            remote(upper, upper, OVER, to_right).start()
+            remote(lower, lower, OVER, to_left).start()
 
     def activate(k, squares, early):
         scale = lax.rsqrt(squares * (1.0 / width) + 0.5)
@@ -313,10 +326,10 @@
     def down(k, ch, qs, i, late=None):
         sub = 2 * ch + qs[0]
         for q in qs:
-            rows_out = mm(hp[core], wd[core, ch, q])
+            rows_out = mm(hp[core], wd[own(ch), q])
             if late is not None and q == qs[0]:
                 d_twin(late, q)
-            rows_out = rows_out + mm(hp[1 - core], wd[1 - core, ch, q])
+            rows_out = rows_out + mm(hp[1 - core], wd[theirs + ch, q])
             tail = rows_out[n_low:2 * n_low, :half] + rows_out[2 * n_low:, half:]
             rets[k, 2 * ch + q, :, :, :cols] = rows_out[:n_low].astype(BF).reshape(n_y, 8, cols)
             rets[k, 2 * ch + q, :, :, cols:] = tail.astype(BF).reshape(n_y, 8, half)
@@ -352,9 +365,6 @@
         mixture = mm(weights, high, 0, 0) + mm(weights, low, 0, 0)
         return (inputs.astype(F32) + mixture).astype(BF)
 
-    def at_cols(c):
-        return pl.ds(pl.multiple_of(c * cols, cols), cols)
-
     pl.semaphore_wait(barrier, greeted)
     w_own(0)
     w_own(1)
@@ -373,39 +383,35 @@
         copy.wait()
     picks = [selection(0)]
     pick_s[...] = picks[0][1]
-    for copy in load_a:
-        copy.wait()
+    load_a.wait()
+    for c in subs:
+        fill(toks, 0, c, mm(picks[0][0], inc[0, :, c * cols:(c + 1) * cols]))
+    spread(toks, tokr, 0, TOK, (1, n_y - 1))
     ring(0)
+    spread(toks, tokr, 0, TOK, (2, n_y - 2))
     told(CROSSED, 2)
     tell(TWIN, sibling)
-    for c in subs:
-        fill(toks, 0, c, mm(picks[0][0], inc[0, c]))
-    ring(1)
     picks.append(selection(1))
     load_c.wait()
     for c in subs:
         fill(cots, 0, c, mm(picks[0][1], cot[0, 0, :, c * cols:(c + 1) * cols]))
-    ring(2)
-
-    @pl.when(jnp.logical_not(first_sec))
-    def _():
-        tell(RING, to_prev)
-
-    spread_all(toks, tokr, 0, TOK)
-    spread_all(cots, cotr, 0, COT)
+    ring(1)
+    spread(toks, tokr, 0, TOK, (3, n_y - 3))
     for c in subs:
         fill(cots, 1, c, mm(picks[1][1], cot[0, 1, :, c * cols:(c + 1) * cols]))
-    spread_all(cots, cotr, 1, COT + 1)
-
-    @pl.when(jnp.logical_not(last_sec))
-    def _():
-        told(NEXT, 1)
-
-    remote(inc.at[0], base, BASE, to_next).start()
-    remote(pick_s, pick_r, PICK, to_next).start()
-    for copy in load_g + load_f:
-        copy.wait()
-    told(TWIN, 1)
+    ring(2)
+    spread(toks, tokr, 0, TOK, (4,))
+
+    @pl.when(jnp.logical_not(first_sec))
+    def _():
+        tell(RING, to_prev)
+
+    spread(cots, cotr, 0, COT, offs)
+    keep(toks, tokr, 0, 0, n_c)
+    for k in range(steps):
+        keep(cots, cotr, k, 0, n_c)
+    load_f.wait()
+    load_g.wait()
 
     items = (
         (dp, (0, 1)), (right, (0,)), (left, (0,)), (right, (1,)), (left, (1,)),
@@ -415,9 +421,36 @@
     def enter(i, blocks):
         ch, qs = items[i]
         for q, block in zip(qs, blocks):
-            inc[1, 2 * ch + q] = block
+            inc[1, :, at_cols(2 * ch + q)] = block
             fill(toks, 1, 2 * ch + q, mm(picks[1][0], block))
-        spread_some(toks, tokr, 1, 2 * ch + qs[0], len(qs), TOK + 1 + i)
+        spread(toks, tokr, 1, TOK + 1 + i, offs, 2 * ch + qs[0], len(qs))
+        keep(toks, tokr, 1, 2 * ch + qs[0], len(qs))
+
+    @pl.when(first_sec)
+    def _():
+        for i, (ch, qs) in enumerate(items):
+            enter(i, [fresh[:, at_cols(2 * ch + q)] for q in qs])
+
+    @pl.when(jnp.logical_not(first_sec))
+    def _():
+        spread(cots, cotr, 1, COT + 1, offs)
+
+    order = (dp, right, left, opp)
+
+    def later(*blocks):
+        @pl.when(first_sec)
+        def _():
+            for i in blocks:
+                spread(cots, cotr, 1, PART + i, offs, 2 * order[i], 2)
+
+
+    @pl.when(jnp.logical_not(last_sec))
+    def _():
+        told(NEXT, 1)
+
+    remote(inc.at[0], base, BASE, to_next).start()
+    remote(pick_s, pick_r, PICK, to_next).start()
+    told(TWIN, 1)
 
     def settle(i):
         ch, qs = items[i]
@@ -425,18 +458,12 @@
         results = []
         for q in qs:
             c = 2 * ch + q
-            results.append(combine(0, c, pick_r[...], base[c]))
+            results.append(combine(0, c, pick_r[...], base[:, at_cols(c)]))
             back[c] = results[-1]
             remote(back.at[c], out.at[0, 0, :, at_cols(c)], BACK, to_prev).start()
         return results
 
     def relay(i):
-        ch, qs = items[i]
-
-        @pl.when(first_sec)
-        def _():
-            enter(i, [fresh[2 * ch + q] for q in qs])
-
         @pl.when(jnp.logical_not(first_sec))
         def _():
             enter(i, settle(i))
@@ -457,16 +484,17 @@
     w_pass(1)
     d_own()
     contract(near, True, (core,))
-    for m in range(2):
-        for i in range(3):
-            w_twin(m, i)
+    w_twin(0, False)
+    w_twin(1, False)
     contract(near, True, (1 - core,))
     w_last(0)
+    contract(far, False, (core,), (0,))
+    w_twin(0, True)
+    contract(far, False, (1 - core,), (0,))
     w_last(1)
-    contract(far, False, (core,))
-    w_twin(0, 3)
-    w_twin(1, 3)
-    contract(far, False, (1 - core,))
+    contract(far, False, (core,), (1,))
+    w_twin(1, True)
+    contract(far, False, (1 - core,), (1,))
     activate(0, squares, False)
     ring(3)
 
@@ -475,50 +503,93 @@
         told(RING, 1)
 
     down(0, dp, (0, 1), 0, "own")
+    later(3)
     d_pass(0)
-    d_twin("right", 0)
+    d_twin("near", 0)
     down(0, right, (0,), 1)
-    d_twin("left", 0)
     down(0, left, (0,), 2)
+    later(1)
     got(base, BASE)
     got(pick_r, PICK)
     d_pass(1)
     relay(0)
-    d_twin("right", 1)
+    d_twin("near", 1)
     down(0, right, (1,), 3)
-    d_twin("left", 1)
     down(0, left, (1,), 4)
+
+    def hand(k, x):
+        remote(
+            cotr.at[k, pl.ds(2 * x, 2)], cotx.at[k, core, dp], CROSS + k, (sec, exp, x)
+        ).start()
+
+    def stay(k):
+        for q in range(2):
+            cotx[k, core, dp, q] = cotr[k, 2 * dp + q]
+
+    def cross(k):
+        got(cotr.at[k, pl.ds(0, n_c), pl.ds(0, n_y - 1)], COT + k)
+        for x in (opp, right, left):
+            hand(k, x)
+        stay(k)
+
+    def cross_part(i):
+        got(cotr.at[1, pl.ds(2 * order[i], 2), pl.ds(0, n_y - 1)], PART + i)
+        if i:
+            hand(1, order[i])
+        else:
+            stay(1)
+
     d_last(0)
     send_hidden(0)
-    for k in range(steps):
-        got(cotr.at[k, pl.ds(0, n_c), pl.ds(0, n_y - 1)], COT + k)
-        for x in (opp, right, left):
-            remote(
-                cotr.at[k, pl.ds(2 * x, 2)], cotx.at[k, core, dp], CROSS + k, (sec, exp, x)
-            ).start()
-        for q in range(2):
-            cotx[k, core, dp, q] = cotr[k, 2 * dp + q]
-    down(0, opp, (0,), 5, "opp")
+    cross(0)
+    relay(1)
     d_last(1)
-    relay(1)
-    down(0, opp, (1,), 6, "opp")
+    down(0, opp, (0,), 5, "far")
+    down(0, opp, (1,), 6, "far")
+    later(2, 0)
+
+    @pl.when(jnp.logical_not(first_sec))
+    def _():
+        cross(1)
+
     relay(2)
+    squares = tok_in(0)
+    contract(parts_of(0), True, (0, 1))
     relay(3)
     relay(4)
-    squares = tok_in(0)
     relay(5)
     relay(6)
-    squares = squares + tok_in(1) + tok_in(2)
-    contract(parts_of(0, 1, 2), True, (0, 1))
+    squares = squares + tok_in(1)
+    contract(parts_of(1), False, (0, 1))
+
+    @pl.when(jnp.logical_not(first_sec))
+    def _():
+        pass_hidden()
+
+    squares = squares + tok_in(2)
+    contract(parts_of(2), False, (0, 1))
     squares = squares + tok_in(3) + tok_in(4)
+    contract(parts_of(3, 4), False, (0, 1))
     squares = squares + tok_in(5)
-    contract(parts_of(3, 4, 5), False, (0, 1))
+    contract(parts_of(5), False, (0, 1))
     squares = squares + tok_in(6)
     contract(parts_of(6), False, (0, 1))
     activate(1, squares, True)
-    order = (dp, right, left, opp)
     for i, ch in enumerate(order):
         down(1, ch, (0, 1), i)
+
+    def results():
+        for i, ch in enumerate(order):
+            landed(1, ch, (0, 1), i)
+            for q in range(2):
+                c = 2 * ch + q
+                out[0, 1, :, at_cols(c)] = combine(1, c, picks[1][1], inc[1, :, at_cols(c)])
+
+    @pl.when(first_sec)
+    def _():
+        pass_hidden()
+        for i in (3, 1, 2, 0):
+            cross_part(i)
 
     @pl.when(first_sec)
     def _():
@@ -529,9 +600,11 @@
     for k in range(steps):
         got(cotx.at[k, core, pl.ds(0, n_d - 1)], CROSS + k)
         remote(cotx.at[k, core], cotx.at[k, core], SWAP + k, sibling).start()
-    for k in range(steps):
         got(cotx.at[k, 0], SWAP + k)
-        got(hidr.at[k, pl.ds(0, CORES * n_d - 1)], HID + k)
+        if k == last:
+            got(hidr.at[k, pl.ds(0, CORES * n_d - 1)], HID + k)
+        else:
+            got(hidr.at[k, pl.ds(0, CORES + 1)], OVER)
         total = 0.0
         for c in range(CORES):
             rows_cot = jnp.concatenate(
@@ -546,35 +619,32 @@
             rows_hid = hidr[k, pl.ds(c * n_d, n_d)].reshape(n_d * CAP * n_y, units)
             total = total + mm(rows_hid, rows_cot, 0, 0)
         grad[0] = total if k == 0 else grad[0] + total
-    for i, ch in enumerate(order):
-        landed(1, ch, (0, 1), i)
-        for q in range(2):
-            c = 2 * ch + q
-            out[0, 1, :, at_cols(c)] = combine(1, c, picks[1][1], inc[1, c])
+        if k == 0:
+
+            @pl.when(first_sec)
+            def _():
+                results()
+
+
+    @pl.when(jnp.logical_not(first_sec))
+    def _():
+        results()
 
     got(back, BACK)
-    for m in range(2):
-        w = mats[m]
-        for i in (0, 1, 4, 5, 6):
-            w_copy(w.at[0, 0], m, i, sibling).wait_send()
-        for i in (2, 3, 7, 8):
-            w_copy(w.at[0, 0, pl.ds(0, part_units)], m, i, sibling).wait_send()
-    for i in (0, 1, 2, 3, 10, 11, 12, 13):
-        d_copy(wd.at[0, 0, 0], i, sibling).wait_send()
-    for i in (4, 5, 6, 7, 14, 15, 16, 17):
-        d_copy(wd.at[0, 0, 0, pl.ds(0, part_units)], i, sibling).wait_send()
-    d_copy(wd.at[0, 0], 8, sibling).wait_send()
-    sent(tokr.at[0, pl.ds(0, n_c), pl.ds(0, n_y - 1)], TOK)
-    for i, (ch, qs) in enumerate(items):
-        sent(tokr.at[1, pl.ds(0, len(qs)), pl.ds(0, n_y - 1)], TOK + 1 + i)
-        sent(rets.at[0, pl.ds(0, len(qs))], RET + i)
-    for i in range(n_d):
-        sent(rets.at[1, pl.ds(0, 2), pl.ds(0, n_y - 1)], RET + 7 + i)
-    for k in range(steps):
-        sent(cotr.at[k, pl.ds(0, n_c), pl.ds(0, n_y - 1)], COT + k)
-        sent(cotx.at[k, 0, pl.ds(0, n_d - 1)], CROSS + k)
-        sent(cotx.at[k, 0], SWAP + k)
-        sent(hidr.at[k, pl.ds(0, CORES * n_d - 1)], HID + k)
+    for m, w in enumerate(mats + (wd,)):
+        ref = w.at[pl.ds(0, CORES * n_d - 1)]
+        pltpu.make_async_remote_copy(
+            src_ref=ref, dst_ref=ref, send_sem=w_send.at[m], recv_sem=w_recv.at[0, 0],
+            device_id=sibling, device_id_type=MESH,
+        ).wait_send()
+    both, every, others = pl.ds(0, steps), pl.ds(0, n_c), pl.ds(0, n_y - 1)
+    sent(tokr.at[both, every, others], TOK)
+    sent(cotr.at[both, every, others], COT)
+    sent(cotx.at[both, 0, pl.ds(0, n_d - 1)], CROSS)
+    sent(cotx.at[both, 0], SWAP)
+    sent(hidr.at[both, pl.ds(0, CORES * n_d - 1)], HID)
+    sent(retr.at[0], RET)
+    sent(retr.at[1, every, others], RET + 7)
     sent(pick_s, PICK)
     sent(base, BASE)
     sent(back, BACK)
@@ -617,16 +687,16 @@
         in_specs=[hbm] * 9,
         out_specs=(held, held),
         scratch_shapes=[
-            vmem(CORES, n_d, units, cols),
-            vmem(CORES, n_d, units, cols),
-            vmem(CORES, n_d, 2, units, sub),
+            vmem(CORES * n_d, units, cols),
+            vmem(CORES * n_d, units, cols),
+            vmem(CORES * n_d, 2, units, sub),
             vmem(1, routes.shape[3], steps, tok_rows, kind=jnp.int32),
             vmem(1, routes.shape[3], steps, tok_rows),
-            vmem(n_c, 1, sub, kind=F32),
+            vmem(1, width, kind=F32),
             vmem(*cotangent.shape),
-            vmem(n_c, tok_rows, sub),
-            vmem(steps, n_c, tok_rows, sub),
-            vmem(n_c, tok_rows, sub),
+            vmem(tok_rows, width),
+            vmem(steps, tok_rows, width),
+            vmem(tok_rows, width),
             vmem(steps, n_c, flight, 8, packed),
             vmem(steps, n_c, n_y, 8, packed),
             vmem(steps, n_c, flight, 8, packed),
@@ -642,12 +712,11 @@
             vmem(used, tok_rows),
             vmem(used, tok_rows),
             vmem(n_c, tok_rows, sub),
-            dma((7 + 3 * n_c,)),
-            dma((2, 9)),
-            dma((2, 9)),
-            dma((18,)),
-            dma((18,)),
-            dma((SEMS,)),
+            dma((10,)),
+            dma((3,)),
+            dma((2, 5)),
+            dma((11,)),
+            dma((SENDS,)),
             dma((SEMS,)),
             pltpu.SemaphoreType.REGULAR((READY,)),
         ],

time: 72.6 us -> 70.8 us (0.975)
  Pallas kernels: 71.9 us -> 69.9 us
    pallas_call x1, Pallas kernels: 70.8 us -> 68.8 us  [local(): pl.pallas_call(functools.partial(kernel, n_s, n_e, n_d, steps), out_shape...]
where the time goes in v1:
time: 70.8 us; the launch traced here: 70.5 us
  Pallas kernels  69.9 us (99%)
    pallas_call x1, Pallas kernels, local(): pl.pallas_call(functools.partial(kernel, n_s, n_e, n_d, steps), out_shape...  68.8 us

profile of v1, /device:TPU:1, one launch (start us, length us, event | category | flops | bytes accessed | tf_op | source)
XLA Modules:
  0.0 70.5 jit_solution(6744098978055029093)
XLA Ops:
  0.6 68.8 %shard_map.104 = (bf16[1,2,64,2048]{3,2,1,0:T(8,128)(2,1)S(1)}, f32[1,352,512]{2,1,0:T(8,128)S(1)}) custom-call(bf16[1,64,2048]{2,1,0:T(8,128)(2,1)} %arr_h.1, bf16[1,64,2048]{2,1,0:T(8,128)(2,1)} %fresh_h.1, s32[1,6,2,64]{3,2,1,0:T(2,128)} %bitcast.2, bf16[1,6,2,64]{3,2,1,0:T(2,128)(2,1)} %bitcast.3, bf16[1,2,64,2048]{3,2,1,0:T(8,128)(2,1)} %cot_h.1, ...), custom_call_target="tpu_custom_call" | custom-call | tf_op jit(solution)/shard_map/pallas_call | solution.py:681
  69.5 1.1 %shard_map.105 = (bf16[1,2,64,2048]{3,2,1,0:T(8,128)(2,1)}, f32[1,352,512]{2,1,0:T(8,128)}) custom-call(bf16[1,2,64,2048]{3,2,1,0:T(8,128)(2,1)S(1)} %get-tuple-element.4.out_in, f32[1,352,512]{2,1,0:T(8,128)S(1)} %get-tuple-element.5.grad_in), custom_call_target="tpu_custom_call" | custom-call | tf_op jit(solution)/shard_map/pallas_call | solution.py:731

commit v2 on v1

--- a/solution.py
+++ b/solution.py
@@ -32,7 +32,7 @@
     wg, wu, wd, routes, gates, gain, cot, fresh, inc, base,
     toks, tokr, cots, cotr, cotx, xg, acc, hid_s, hidr, hp, rets, retr,
     pick_s, pick_r, back,
-    load_sems, w_send, w_recv, d_recv, send_sems, recv_sems, ready,
+    load_sems, w_send, g_recv, h_recv, send_sems, recv_sems, ready,
 ):
     sec = lax.axis_index("section")
     exp = lax.axis_index("expert")
@@ -120,7 +120,8 @@
     def own(x):
         return core * n_d + x
 
-    load_w = [load(wg_h.at[0], wg.at[mine]), load(wu_h.at[0], wu.at[mine])]
+    load_w = load(wg_h.at[0], wg.at[mine])
+    load_u = [load(wu_h.at[0, :, piece(q)], wu.at[mine, q]) for q in range(2)]
     load_r = [load(routes_h, routes), load(gates_h, gates)]
     load_a = load(arr_h.at[0], inc.at[0])
     load_d = [load(wd_h.at[0, :, piece(q)], wd.at[mine, q]) for q in range(2)]
@@ -146,74 +147,76 @@
     def sent(ref, sem):
         remote(ref, ref, sem, sibling).wait_send()
 
-    mats = (wg, wu)
-
-    def w_copy(ref, m, i, target):
+    def g_copy(ref, i, target):
         return pltpu.make_async_remote_copy(
-            src_ref=ref, dst_ref=ref, send_sem=w_send.at[m], recv_sem=w_recv.at[m, i],
+            src_ref=ref, dst_ref=ref, send_sem=w_send.at[0], recv_sem=g_recv.at[i],
             device_id=target, device_id_type=MESH,
         )
 
-    def w_own(m):
-        load_w[m].wait()
-        ref = mats[m].at[mine]
-        w_copy(ref, m, 0, to_right).start()
-        w_copy(ref, m, 1, to_left).start()
-        w_copy(ref, m, 3, sibling).start()
-
-    def w_pass(m):
-        w = mats[m]
-        w_copy(w.at[own(left)], m, 0, sibling).wait_recv()
-        w_copy(w.at[own(left), pl.ds(0, part_units)], m, 2, to_right).start()
-        w_copy(w.at[own(left)], m, 3, sibling).start()
-        w_copy(w.at[own(right)], m, 1, sibling).wait_recv()
-        w_copy(w.at[own(right), pl.ds(part_units, part_units)], m, 2, to_left).start()
-        w_copy(w.at[own(right)], m, 3, sibling).start()
-
-    def w_last(m):
-        ref = mats[m].at[own(opp)]
-        w_copy(ref, m, 2, sibling).wait_recv()
-        w_copy(ref, m, 4, sibling).start()
-
-    def w_twin(m, far_one):
+    def g_own():
+        load_w.wait()
+        ref = wg.at[mine]
+        g_copy(ref, 0, to_right).start()
+        g_copy(ref, 1, to_left).start()
+        g_copy(ref, 3, sibling).start()
+
+    def g_pass():
+        g_copy(wg.at[own(left)], 0, sibling).wait_recv()
+        g_copy(wg.at[own(left), pl.ds(0, part_units)], 2, to_right).start()
+        g_copy(wg.at[own(left)], 3, sibling).start()
+        g_copy(wg.at[own(right)], 1, sibling).wait_recv()
+        g_copy(wg.at[own(right), pl.ds(part_units, part_units)], 2, to_left).start()
+        g_copy(wg.at[own(right)], 3, sibling).start()
+
+    def g_last():
+        ref = wg.at[own(opp)]
+        g_copy(ref, 2, sibling).wait_recv()
+        g_copy(ref, 4, sibling).start()
+
+    def g_twin(far_one):
         if far_one:
-            w_copy(mats[m].at[theirs + opp], m, 4, sibling).wait_recv()
+            g_copy(wg.at[theirs + opp], 4, sibling).wait_recv()
         else:
-            w_copy(mats[m].at[pl.ds(theirs, 3)], m, 3, sibling).wait_recv()
-
-    def d_copy(ref, i, target):
+            g_copy(wg.at[pl.ds(theirs, 3)], 3, sibling).wait_recv()
+
+    halves = (wu, wd)
+
+    def h_copy(ref, m, i, target):
         return pltpu.make_async_remote_copy(
-            src_ref=ref, dst_ref=ref, send_sem=w_send.at[2], recv_sem=d_recv.at[i],
+            src_ref=ref, dst_ref=ref, send_sem=w_send.at[1 + m], recv_sem=h_recv.at[m, i],
             device_id=target, device_id_type=MESH,
         )
 
-    def d_own():
+    def h_own(m):
+        w = halves[m]
         for q in range(2):
-            load_d[q].wait()
-            d_copy(wd.at[mine, q], q, to_right).start()
-            d_copy(wd.at[mine, q], 2 + q, to_left).start()
-        d_copy(wd.at[mine], 6, sibling).start()
-
-    def d_pass(q):
-        d_copy(wd.at[own(left), q], q, sibling).wait_recv()
-        d_copy(wd.at[own(left), q, pl.ds(0, part_units)], 4 + q, to_right).start()
-        d_copy(wd.at[own(left), q], 7 + q, sibling).start()
-        d_copy(wd.at[own(right), q], 2 + q, sibling).wait_recv()
-        d_copy(wd.at[own(right), q, pl.ds(part_units, part_units)], 4 + q, to_left).start()
-        d_copy(wd.at[own(right), q], 7 + q, sibling).start()
-
-    def d_last(q):
-        ref = wd.at[own(opp), q]
-        d_copy(ref, 4 + q, sibling).wait_recv()
-        d_copy(ref, 9 + q, sibling).start()
-
-    def d_twin(name, q):
+            (load_u, load_d)[m][q].wait()
+            h_copy(w.at[mine, q], m, q, to_right).start()
+            h_copy(w.at[mine, q], m, 2 + q, to_left).start()
+        h_copy(w.at[mine], m, 6, sibling).start()
+
+    def h_pass(m, q):
+        w = halves[m]
+        h_copy(w.at[own(left), q], m, q, sibling).wait_recv()
+        h_copy(w.at[own(left), q, pl.ds(0, part_units)], m, 4 + q, to_right).start()
+        h_copy(w.at[own(left), q], m, 7 + q, sibling).start()
+        h_copy(w.at[own(right), q], m, 2 + q, sibling).wait_recv()
+        h_copy(w.at[own(right), q, pl.ds(part_units, part_units)], m, 4 + q, to_left).start()
+        h_copy(w.at[own(right), q], m, 7 + q, sibling).start()
+
+    def h_last(m, q):
+        ref = halves[m].at[own(opp), q]
+        h_copy(ref, m, 4 + q, sibling).wait_recv()
+        h_copy(ref, m, 9 + q, sibling).start()
+
+    def h_twin(m, name, q):
+        w = halves[m]
         if name == "own":
-            d_copy(wd.at[theirs + dp], 6, sibling).wait_recv()
+            h_copy(w.at[theirs + dp], m, 6, sibling).wait_recv()
         elif name == "near":
-            d_copy(wd.at[theirs + dp], 7 + q, sibling).wait_recv()
+            h_copy(w.at[theirs + dp], m, 7 + q, sibling).wait_recv()
         else:
-            d_copy(wd.at[theirs + opp, q], 9 + q, sibling).wait_recv()
+            h_copy(w.at[theirs + opp, q], m, 9 + q, sibling).wait_recv()
 
     lane = lax.broadcasted_iota(jnp.int32, (used, rows), 0)
     lane_expert = lane >> 4
@@ -287,11 +290,11 @@
     def contract(parts, first, cores, which=(0, 1)):
         for c in cores:
             for i in which:
-                w = mats[i]
-                total = sum(
-                    mm(xg[2 * ch + q], w[c * n_d + ch, :, q * cols:(q + 1) * cols], 1, 1)
-                    for ch, q in parts
-                )
+                total = 0.0
+                for ch, q in parts:
+                    at = c * n_d + ch
+                    w = wu[at, q] if i else wg[at, :, q * cols:(q + 1) * cols]
+                    total = total + mm(xg[2 * ch + q], w, 1, 1)
                 acc[i, c] = total if first else acc[i, c] + total
 
     def send_hidden(k):
@@ -328,7 +331,7 @@
         for q in qs:
             rows_out = mm(hp[core], wd[own(ch), q])
             if late is not None and q == qs[0]:
-                d_twin(late, q)
+                h_twin(1, late, q)
             rows_out = rows_out + mm(hp[1 - core], wd[theirs + ch, q])
             tail = rows_out[n_low:2 * n_low, :half] + rows_out[2 * n_low:, half:]
             rets[k, 2 * ch + q, :, :, :cols] = rows_out[:n_low].astype(BF).reshape(n_y, 8, cols)
@@ -366,8 +369,8 @@
         return (inputs.astype(F32) + mixture).astype(BF)
 
     pl.semaphore_wait(barrier, greeted)
-    w_own(0)
-    w_own(1)
+    g_own()
+    h_own(0)
     tell(NEAR, above, below)
     tell(CROSSED, to_right, to_left)
 
@@ -478,23 +481,30 @@
 
     near = parts_of(0, 1, 2, 3, 4)
     far = parts_of(5, 6)
-    w_pass(0)
+    g_pass()
     got(tokr.at[0, pl.ds(0, n_c), pl.ds(0, n_y - 1)], TOK)
     squares = sum(prepare(0, c) for c in subs)
-    w_pass(1)
-    d_own()
+    h_pass(0, 0)
+    h_pass(0, 1)
+    h_own(1)
     contract(near, True, (core,))
-    w_twin(0, False)
-    w_twin(1, False)
+    g_twin(False)
+    h_twin(0, "own", 0)
+    h_twin(0, "near", 0)
+    h_twin(0, "near", 1)
     contract(near, True, (1 - core,))
-    w_last(0)
+    g_last()
     contract(far, False, (core,), (0,))
-    w_twin(0, True)
+    g_twin(True)
     contract(far, False, (1 - core,), (0,))
-    w_last(1)
-    contract(far, False, (core,), (1,))
-    w_twin(1, True)
-    contract(far, False, (1 - core,), (1,))
+    h_last(0, 0)
+    contract(parts_of(5), False, (core,), (1,))
+    h_last(0, 1)
+    contract(parts_of(6), False, (core,), (1,))
+    h_twin(0, "far", 0)
+    contract(parts_of(5), False, (1 - core,), (1,))
+    h_twin(0, "far", 1)
+    contract(parts_of(6), False, (1 - core,), (1,))
     activate(0, squares, False)
     ring(3)
 
@@ -504,16 +514,16 @@
 
     down(0, dp, (0, 1), 0, "own")
     later(3)
-    d_pass(0)
-    d_twin("near", 0)
+    h_pass(1, 0)
+    h_twin(1, "near", 0)
     down(0, right, (0,), 1)
     down(0, left, (0,), 2)
     later(1)
     got(base, BASE)
     got(pick_r, PICK)
-    d_pass(1)
+    h_pass(1, 1)
     relay(0)
-    d_twin("near", 1)
+    h_twin(1, "near", 1)
     down(0, right, (1,), 3)
     down(0, left, (1,), 4)
 
@@ -539,11 +549,11 @@
         else:
             stay(1)
 
-    d_last(0)
+    h_last(1, 0)
     send_hidden(0)
     cross(0)
     relay(1)
-    d_last(1)
+    h_last(1, 1)
     down(0, opp, (0,), 5, "far")
     down(0, opp, (1,), 6, "far")
     later(2, 0)
@@ -575,13 +585,14 @@
     squares = squares + tok_in(6)
     contract(parts_of(6), False, (0, 1))
     activate(1, squares, True)
-    for i, ch in enumerate(order):
-        down(1, ch, (0, 1), i)
+    ends = tuple((ch, (0, 1)) for ch in order)
+    for i, (ch, qs) in enumerate(ends):
+        down(1, ch, qs, i)
 
     def results():
-        for i, ch in enumerate(order):
-            landed(1, ch, (0, 1), i)
-            for q in range(2):
+        for i, (ch, qs) in enumerate(ends):
+            landed(1, ch, qs, i)
+            for q in qs:
                 c = 2 * ch + q
                 out[0, 1, :, at_cols(c)] = combine(1, c, picks[1][1], inc[1, :, at_cols(c)])
 
@@ -631,10 +642,10 @@
         results()
 
     got(back, BACK)
-    for m, w in enumerate(mats + (wd,)):
+    for m, w in enumerate((wg, wu, wd)):
         ref = w.at[pl.ds(0, CORES * n_d - 1)]
         pltpu.make_async_remote_copy(
-            src_ref=ref, dst_ref=ref, send_sem=w_send.at[m], recv_sem=w_recv.at[0, 0],
+            src_ref=ref, dst_ref=ref, send_sem=w_send.at[m], recv_sem=g_recv.at[0],
             device_id=sibling, device_id_type=MESH,
         ).wait_send()
     both, every, others = pl.ds(0, steps), pl.ds(0, n_c), pl.ds(0, n_y - 1)
@@ -688,7 +699,7 @@
         out_specs=(held, held),
         scratch_shapes=[
             vmem(CORES * n_d, units, cols),
-            vmem(CORES * n_d, units, cols),
+            vmem(CORES * n_d, 2, units, sub),
             vmem(CORES * n_d, 2, units, sub),
             vmem(1, routes.shape[3], steps, tok_rows, kind=jnp.int32),
             vmem(1, routes.shape[3], steps, tok_rows),
@@ -712,10 +723,10 @@
             vmem(used, tok_rows),
             vmem(used, tok_rows),
             vmem(n_c, tok_rows, sub),
-            dma((10,)),
+            dma((11,)),
             dma((3,)),
-            dma((2, 5)),
-            dma((11,)),
+            dma((5,)),
+            dma((2, 11)),
             dma((SENDS,)),
             dma((SEMS,)),
             pltpu.SemaphoreType.REGULAR((READY,)),

time: 70.8 us -> 70.9 us (level)
  no operation moved by 1% of the time
where the time goes in v2:
time: 70.9 us; the launch traced here: 70.6 us
  Pallas kernels  69.9 us (99%)
    pallas_call x1, Pallas kernels, local(): pl.pallas_call(functools.partial(kernel, n_s, n_e, n_d, steps), out_shape...  68.9 us

profile of v2, /device:TPU:1, one launch (start us, length us, event | category | flops | bytes accessed | tf_op | source)
XLA Modules:
  0.0 70.6 jit_solution(16347773652035756395)
XLA Ops:
  0.6 68.9 %shard_map.104 = (bf16[1,2,64,2048]{3,2,1,0:T(8,128)(2,1)S(1)}, f32[1,352,512]{2,1,0:T(8,128)S(1)}) custom-call(bf16[1,64,2048]{2,1,0:T(8,128)(2,1)} %arr_h.1, bf16[1,64,2048]{2,1,0:T(8,128)(2,1)} %fresh_h.1, s32[1,6,2,64]{3,2,1,0:T(2,128)} %bitcast.2, bf16[1,6,2,64]{3,2,1,0:T(2,128)(2,1)} %bitcast.3, bf16[1,2,64,2048]{3,2,1,0:T(8,128)(2,1)} %cot_h.1, ...), custom_call_target="tpu_custom_call" | custom-call | tf_op jit(solution)/shard_map/pallas_call | solution.py:692
  69.5 1.1 %shard_map.105 = (bf16[1,2,64,2048]{3,2,1,0:T(8,128)(2,1)}, f32[1,352,512]{2,1,0:T(8,128)}) custom-call(bf16[1,2,64,2048]{3,2,1,0:T(8,128)(2,1)S(1)} %get-tuple-element.4.out_in, f32[1,352,512]{2,1,0:T(8,128)S(1)} %get-tuple-element.5.grad_in), custom_call_target="tpu_custom_call" | custom-call | tf_op jit(solution)/shard_map/pallas_call | solution.py:742
